TPU v7x, 32 devices: a whole 2x2x4 slice. The times are simulated.
32 devices in a mesh: seq: 8 (over y, x, core), head: 4 (over z).
Axes of the slice: x: 2, y: 2, z: 4, core: 2. Of those that a mesh axis runs over, the one named last changes fastest.
Arguments:
- latent: bfloat16 [8, 1024, 2048], P('seq', None, 'head'), may hold values from -6 to 6
- modulation: float32 [9, 2048], replicated, may hold values from -3 to 3
- spatial_qkv: bfloat16 [3, 2048, 2048], P(None, None, 'head')
- spatial_out: bfloat16 [2048, 2048], P('head'), may hold values from -0.125 to 0.125
- temporal_qkv: bfloat16 [3, 2048, 2048], P(None, None, 'head')
- temporal_out: bfloat16 [2048, 2048], P('head'), may hold values from -0.125 to 0.125
- hidden_weight: bfloat16 [2048, 8192], P(None, 'head'), may hold values from -0.125 to 0.125
- output_weight: bfloat16 [8192, 2048], P('head'), may hold values from -0.0625 to 0.0625
Outputs:
- block_out: bfloat16 [8, 1024, 2048], P(None, 'seq', 'head')
All inputs are finite; a program needn't handle non-finite values.
Results may differ from a plain program's by a relative error of at most 0.009.
Values may be sent and summed in bfloat16 or wider, within the bound.
A program may use at most 128 MiB of HBM per device.

v0:
```python
import jax
import jax.numpy as jnp
from jax import lax
from jax.sharding import PartitionSpec as P

HD = 64


def layer_norm(values):
    average = jnp.mean(values, axis=-1, keepdims=True)
    centred = values - average
    variance = jnp.mean(centred * centred, axis=-1, keepdims=True)
    return centred * lax.rsqrt(variance + 1e-06)


def modulate(stream, modulation, offset):
    normed = layer_norm(stream.astype(jnp.float32))
    return (normed * (1.0 + modulation[offset + 1]) + modulation[offset]).astype(jnp.bfloat16)


def attend(query, keys, values):
    scores = jnp.einsum(
        "glhd,gmhd->ghlm", query, keys, preferred_element_type=jnp.float32
    ) * HD ** (-0.5)
    attn_weights = jax.nn.softmax(scores, axis=-1).astype(jnp.bfloat16)
    return jnp.einsum(
        "ghlm,gmhd->glhd", attn_weights, values, preferred_element_type=jnp.float32
    ).astype(jnp.bfloat16)


def project_three(normed, weights):
    return [
        jnp.dot(normed, weights[member], preferred_element_type=jnp.float32).astype(jnp.bfloat16)
        for member in range(3)
    ]


def column_adder(columns, portion):
    return jnp.dot(portion, columns, preferred_element_type=jnp.float32)


def per_device(
    latent,
    modulation,
    spatial_qkv,
    spatial_out,
    temporal_qkv,
    temporal_out,
    hidden_weight,
    output_weight,
):
    width_local = latent.shape[2]
    heads_local = width_local // HD
    anchor = lax.axis_index("head") * width_local
    local_rows = lax.dynamic_slice_in_dim(modulation, anchor, width_local, 1)
    full_spatial = lax.all_gather(latent, "head", axis=2, tiled=True)
    normed = modulate(full_spatial, modulation, 0)
    frames_local = latent.shape[0]
    patches = latent.shape[1]
    query, keys, values = [
        member.reshape(frames_local, patches, heads_local, HD)
        for member in project_three(normed, spatial_qkv)
    ]
    spatial = lax.map(
        lambda triple: attend(triple[0][None], triple[1][None], triple[2][None])[0],
        (query, keys, values),
    )
    spatial = spatial.reshape(frames_local, patches, width_local)
    columns = lax.all_to_all(spatial_out, "head", split_axis=1, concat_axis=0, tiled=True)
    reduced = column_adder(columns, lax.all_gather(spatial, "head", axis=2, tiled=True))
    stream_one = (latent.astype(jnp.float32) + local_rows[2] * reduced).astype(jnp.bfloat16)
    full_stream = lax.all_gather(stream_one, "head", axis=2, tiled=True)
    normed = modulate(full_stream, modulation, 3)
    stacked = jnp.stack(project_three(normed, temporal_qkv), axis=2)
    moved, stream_temporal = (
        lax.all_to_all(stacked, "seq", split_axis=1, concat_axis=0, tiled=True),
        lax.all_to_all(stream_one, "seq", split_axis=1, concat_axis=0, tiled=True),
    )
    query, keys, values = (moved[:, :, 0], moved[:, :, 1], moved[:, :, 2])
    frames = stream_temporal.shape[0]
    patches_local = stream_temporal.shape[1]

    def to_groups(tensor):
        return jnp.transpose(tensor.reshape(frames, patches_local, heads_local, HD), (1, 0, 2, 3))

    temporal = attend(to_groups(query), to_groups(keys), to_groups(values))
    temporal = jnp.transpose(temporal, (1, 0, 2, 3)).reshape(frames, patches_local, width_local)
    columns = lax.all_to_all(temporal_out, "head", split_axis=1, concat_axis=0, tiled=True)
    reduced = column_adder(columns, lax.all_gather(temporal, "head", axis=2, tiled=True))
    stream_two = (stream_temporal.astype(jnp.float32) + local_rows[5] * reduced).astype(
        jnp.bfloat16
    )
    full_two = lax.all_gather(stream_two, "head", axis=2, tiled=True)
    normed = modulate(full_two, modulation, 6)
    pre_act = jnp.dot(normed, hidden_weight, preferred_element_type=jnp.float32)
    hidden = jax.nn.gelu(pre_act, approximate=True).astype(jnp.bfloat16)
    partial_sums = jnp.dot(hidden, output_weight, preferred_element_type=jnp.float32)
    reduced = lax.psum_scatter(partial_sums, "head", scatter_dimension=2, tiled=True)
    return (stream_two.astype(jnp.float32) + local_rows[8] * reduced).astype(jnp.bfloat16)


def solution(mesh):
    in_specs = (
        P("seq", None, "head"),
        P(),
        P(None, None, "head"),
        P("head", None),
        P(None, None, "head"),
        P("head", None),
        P(None, "head"),
        P("head", None),
    )
    out_specs = P(None, "seq", "head")
    return jax.shard_map(
        per_device, mesh=mesh, in_specs=in_specs, out_specs=out_specs, check_vma=False
    )
```

profile of v0, /device:TPU:0, one launch (start us, length us, event | category | flops | bytes accessed | tf_op | source)
XLA Modules:
  0.0 838.2 jit_solution(230585978647317202)
XLA Ops:
  6.5 0.7 all-gather.6.cloned.1.call-update
  7.3 1.7 slice_add_fusion
  9.0 83.4 %all-gather.6.cloned.1.call-done = bf16[1,1024,2048]{2,1,0:T(8,128)(2,1)} async-done(((bf16[1,1024,512]{2,1,0:T(8,128)(2,1)}), bf16[1,1024,2048]{2,1,0:T(8,128)(2,1)}) %all-gather.6.cloned.1.call-update) | async-done | bytes 4194320 | tf_op jit(solution)/shard_map/all_gather | solution.py:56
  92.4 3.0 convert_reduce_fusion.2
  95.4 0.5 copy-done
  95.8 1.2 fusion.21
  97.1 1.9 fusion.42
  99.0 2.4 fusion.95
  101.4 2.4 fusion.98
  103.8 2.4 fusion.101
  106.3 14.6 %fusion.131 = (f32[8,1024]{1,0:T(8,128)S(1)}, f32[8,1024,1024]{1,2,0:T(8,128)}) fusion(bf16[1024,8,64]{0,2,1:T(8,128)(2,1)S(1)} %bitcast.158, bf16[1024,8,64]{0,2,1:T(8,128)(2,1)S(1)} %bitcast.159), kind=kOutput, calls=%fused_computation.121 | convolution fusion | flops 1098908672 | bytes 35684352 | tf_op jit(solution)/shard_map/while/body/eval_jaxpr/sub | solution.py:25
  120.9 13.4 %fusion.113 = bf16[8,64,1024]{2,1,0:T(8,128)(2,1)} fusion(bf16[1024,8,64]{0,2,1:T(8,128)(2,1)S(1)} %bitcast.157, f32[8,1024,1024]{1,2,0:T(8,128)} %get-tuple-element.33, f32[8,1024]{1,0:T(8,128)S(1)} %get-tuple-element.32), kind=kOutput, calls=%fused_computation.100 | convolution fusion | flops 1091043328 | bytes 35684352 | tf_op jit(solution)/shard_map/while/body/eval_jaxpr/ghlm,gmhd->glhd/dot_general | solution.py:26
  134.3 2.5 copy.49
  136.8 3.8 all-to-all-start
  140.9 0.9 fusion.130
  141.7 100.5 %all-to-all-done = bf16[512,4,512]{0,2,1:T(8,128)(2,1)S(1)} async-done(((bf16[512,4,512]{0,2,1:T(8,128)(2,1)}), bf16[512,4,512]{0,2,1:T(8,128)(2,1)S(1)}, u32[]{:S(2)}, u32[]{:S(2)}) %all-to-all-start) | async-done | bytes 2097184 | tf_op jit(solution)/shard_map/all_to_all | solution.py:69
  242.2 2.4 copy.50
  244.6 12.0 %all-gather.8.cloned.1.call-done = bf16[1,1024,2048]{1,2,0:T(8,128)(2,1)} async-done(((bf16[1,1024,512]{1,2,0:T(8,128)(2,1)}), bf16[1,1024,2048]{1,2,0:T(8,128)(2,1)}) %all-gather.8.cloned.1.call-update) | async-done | bytes 4194320 | tf_op jit(solution)/shard_map/all_gather | solution.py:70
  256.6 6.2 fusion.76
  262.9 79.9 %all-gather.10.cloned.1.call-done = bf16[1,1024,2048]{2,1,0:T(8,128)(2,1)} async-done(((bf16[1,1024,512]{2,1,0:T(8,128)(2,1)}), bf16[1,1024,2048]{2,1,0:T(8,128)(2,1)}) %all-gather.10.cloned.1.call-update) | async-done | bytes 4194320 | tf_op jit(solution)/shard_map/all_gather | solution.py:72
  342.8 3.0 convert_reduce_fusion.1
  345.8 0.5 copy-done.1
  346.3 1.2 fusion.17
  347.5 1.9 fusion.43
  349.4 0.4 slice-done.3
  349.8 2.3 fusion.114
  352.1 2.3 fusion.117
  354.4 2.3 fusion.120
  356.7 0.3 pad_maximum_fusion
  357.1 2.7 copy.52
  359.8 52.9 %all_to_all.59 = bf16[1,1024,3,512]{3,2,0,1:T(4,128)(2,1)S(1)} all-to-all(bf16[1,1024,3,512]{3,2,0,1:T(4,128)(2,1)S(1)} %copy.52), channel_id=1, replica_groups=mesh['seq'=8,'head'=4] {'seq'}, dimensions={1} | all-to-all | bytes 6291456 | tf_op jit(solution)/shard_map/all_to_all | solution.py:76
  412.7 0.8 copy.53
  413.5 1.5 fusion.129
  415.0 0.7 copy.58
  415.7 3.0 copy.59
  418.7 1.6 copy.56
  420.3 3.8 copy.57
  424.1 2.8 fusion.66
  426.9 4.6 fusion.132
  431.5 0.7 copy.54
  432.2 3.0 copy.55
  435.2 4.2 convert_bitcast_fusion
  439.4 3.3 copy.61
  442.7 1.5 copy.62
  444.3 1.6 copy.71
  445.9 0.5 broadcast.127
  446.4 7.0 reduce.8
  453.5 1.6 reshape.197
  455.1 3.6 all-to-all-start.1
  458.6 1.6 copy.70
  460.2 13.7 %all-to-all-done.1 = bf16[8,2,32768]{2,1,0:T(2,128)(2,1)S(1)} async-done(((bf16[8,2,32768]{2,1,0:T(2,128)(2,1)}), bf16[8,2,32768]{2,1,0:T(2,128)(2,1)S(1)}, u32[]{:S(2)}, u32[]{:S(2)}) %all-to-all-start.1) | async-done | bytes 1048608 | tf_op jit(solution)/shard_map/all_to_all | solution.py:77
  473.9 4.4 all-to-all-start.3
  478.4 1.1 reshape.198
  479.5 1.6 copy.66
  481.1 85.2 %all-to-all-done.3 = bf16[512,4,512]{2,0,1:T(8,128)(2,1)} async-done(((bf16[512,4,512]{2,0,1:T(8,128)(2,1)}), bf16[512,4,512]{2,0,1:T(8,128)(2,1)}, u32[]{:S(2)}, u32[]{:S(2)}) %all-to-all-start.3) | async-done | bytes 2097184 | tf_op jit(solution)/shard_map/all_to_all | solution.py:88
  566.2 6.7 add_convert_fusion.1
  573.0 0.3 reduce-scatter.2.cloned.1.call-start
  573.3 79.0 %all-gather.14.cloned.1.call-done = bf16[8,128,2048]{2,1,0:T(8,128)(2,1)} async-done(((bf16[8,128,512]{2,1,0:T(8,128)(2,1)}), bf16[8,128,2048]{2,1,0:T(8,128)(2,1)}) %all-gather.14.cloned.1.call-update) | async-done | bytes 4194320 | tf_op jit(solution)/shard_map/all_gather | solution.py:93
  652.3 3.0 convert_reduce_fusion
  655.3 0.5 copy-done.2
  655.8 1.2 fusion.13
  657.0 27.8 %fusion.33 = f32[8,128,2048]{2,1,0:T(8,128)} fusion(bf16[2048,2048]{1,0:T(8,128)(2,1)} %param.15, bf16[2048,2048]{1,0:T(8,128)(2,1)} %param.14, bf16[8,128,2048]{2,1,0:T(8,128)(2,1)} %all-gather.14.cloned.1.call-done, f32[2048]{0:T(1024)S(1)} %bitcast.150, f32[2048]{0:T(1024)S(1)} %bitcast.149, f32[8,128]{1,0:T(8,128)S(1)} %add_rsqrt_fusion, ...), kind=kOutput, calls=%fused_computation.41 | convolution fusion | flops 17211326464 | bytes 29384704 | tf_op jit(solution)/shard_map/dot_general | solution.py:97
  684.8 143.3 %reduce-scatter.2.cloned.1.call-done = f32[8,128,512]{2,1,0:T(8,128)} async-done(((f32[8,128,2048]{2,1,0:T(8,128)}), f32[8,128,512]{2,1,0:T(8,128)}) %reduce-scatter.2.cloned.1.call-update) | async-done | bytes 2097168 | tf_op jit(solution)/shard_map/reduce_scatter | solution.py:98
  828.1 2.9 add_convert_fusion
  (45 shorter events, 0.5 us)
Async XLA Ops:
  6.5 85.9 %all-gather.6.cloned.1.call-start = ((), (), s32[]{:S(2)}) async-start(), calls=%async_computation.5 | async-start | bytes 5242880 | tf_op jit(solution)/shard_map/all_gather | solution.py:56
  7.3 249.4 %all-gather.8.cloned.1.call-start = ((), (), s32[]{:S(2)}) async-start(), calls=%async_computation.6 | async-start | bytes 5242880 | tf_op jit(solution)/shard_map/all_gather | solution.py:70
  92.4 3.4 copy-start
  95.8 3.1 slice-start
  97.1 1.9 slice-start.1
  120.9 13.4 %copy-start.6 = (bf16[512,2048]{1,0:T(8,128)(2,1)S(1)}, bf16[512,2048]{1,0:T(8,128)(2,1)}, u32[]{:S(2)}) copy-start(bf16[512,2048]{1,0:T(8,128)(2,1)} %param.11) | copy-start | bytes 6291460
  136.8 119.8 %copy-start.8 = (bf16[1,1024,512]{2,1,0:T(8,128)(2,1)S(1)}, bf16[1,1024,512]{2,1,0:T(8,128)(2,1)}, u32[]{:S(2)}) copy-start(bf16[1,1024,512]{2,1,0:T(8,128)(2,1)} %param.8) | copy-start | bytes 3145732
  136.8 105.4 %all-to-all-start = ((bf16[512,4,512]{0,2,1:T(8,128)(2,1)}), bf16[512,4,512]{0,2,1:T(8,128)(2,1)S(1)}, u32[]{:S(2)}, u32[]{:S(2)}) async-start(bf16[512,4,512]{0,2,1:T(8,128)(2,1)} %bitcast.133), calls=%async_computation | async-start | bytes 4194304 | tf_op jit(solution)/shard_map/all_to_all | solution.py:69
  140.6 202.2 %all-gather.10.cloned.1.call-start = ((), (), s32[]{:S(2)}) async-start(), calls=%async_computation.7 | async-start | bytes 5242880 | tf_op jit(solution)/shard_map/all_gather | solution.py:72
  262.8 303.4 %all-gather.12.cloned.1.call-start = ((), (), s32[]{:S(2)}) async-start(), calls=%async_computation.8 | async-start | bytes 5242880 | tf_op jit(solution)/shard_map/all_gather | solution.py:89
  342.8 3.4 copy-start.1
  346.3 3.1 slice-start.2
  347.5 2.3 slice-start.3
  426.9 4.7 copy-start.5
  439.4 4.8 copy-start.3
  453.5 5.2 copy-start.7
  455.1 18.9 %all-to-all-start.1 = ((bf16[8,2,32768]{2,1,0:T(2,128)(2,1)}), bf16[8,2,32768]{2,1,0:T(2,128)(2,1)S(1)}, u32[]{:S(2)}, u32[]{:S(2)}) async-start(bf16[8,2,32768]{2,1,0:T(2,128)(2,1)} %reshape.197), calls=%async_computation.1 | async-start | bytes 2097152 | tf_op jit(solution)/shard_map/all_to_all | solution.py:77
  473.9 92.3 %all-to-all-start.3 = ((bf16[512,4,512]{2,0,1:T(8,128)(2,1)}), bf16[512,4,512]{2,0,1:T(8,128)(2,1)}, u32[]{:S(2)}, u32[]{:S(2)}) async-start(bf16[512,4,512]{2,0,1:T(8,128)(2,1)} %bitcast.129), calls=%async_computation.3 | async-start | bytes 4194304 | tf_op jit(solution)/shard_map/all_to_all | solution.py:88
  478.4 173.9 %all-gather.14.cloned.1.call-start = ((), (), s32[]{:S(2)}) async-start(), calls=%async_computation.9 | async-start | bytes 5242880 | tf_op jit(solution)/shard_map/all_gather | solution.py:93
  573.0 84.0 %copy-start.10 = (f32[1,2048]{1,0:T(1,128)S(1)}, f32[1,2048]{1,0:T(1,128)}, u32[]{:S(2)}) copy-start(f32[1,2048]{1,0:T(1,128)} %get-tuple-element.31) | copy-start | bytes 24580
  573.0 84.0 %copy-start.9 = (f32[1,2048]{1,0:T(1,128)S(1)}, f32[1,2048]{1,0:T(1,128)}, u32[]{:S(2)}) copy-start(f32[1,2048]{1,0:T(1,128)} %get-tuple-element.26) | copy-start | bytes 24580
  573.0 255.1 %reduce-scatter.2.cloned.1.call-start = ((), (), s32[]{:S(2)}) async-start(), calls=%async_computation.10 | async-start | bytes 10485760 | tf_op jit(solution)/shard_map/reduce_scatter | solution.py:98
  652.3 3.4 copy-start.2
  684.8 143.3 %copy-start.4 = (bf16[8,128,512]{2,1,0:T(8,128)(2,1)S(1)}, bf16[8,128,512]{2,1,0:T(8,128)(2,1)}, u32[]{:S(2)}) copy-start(bf16[8,128,512]{2,1,0:T(8,128)(2,1)} %add_convert_fusion.1) | copy-start | bytes 3145732
Sparse Core Ops, SparseCore 0:
  8.9 83.4 all-gather.5
  134.4 122.1 all-gather.7
  263.0 79.7 all-gather.9
  444.4 121.0 all-gather.11
  573.1 79.1 all-gather.13
  685.0 143.0 reduce-scatter.1
where the time goes:
time: 849 us; the launch traced here: 838 us
  waiting for transfers between devices  598 us (70%)
  matrix products  90 us (11%)
  blocking collectives  52.9 us (6%)
  local copies, waits for them, and re-layouts  38 us (4%)
  other arithmetic  33 us (4%)
  between operations  14.2 us (2%)
  starting transfers between devices  12.4 us (1%)
    reduce_scatter x1, waiting for transfers between devices, per_device(): lax.psum_scatter(partial_sums, 'head', scatter_dimension=2, tiled=True)  143 us
    all_to_all x1, waiting for transfers between devices, per_device(): lax.all_to_all(spatial_out, 'head', split_axis=1, concat_axis=0, tiled=True)  100 us
    all_to_all x1, waiting for transfers between devices, per_device(): lax.all_to_all(temporal_out, 'head', split_axis=1, concat_axis=0, tiled=T...  85.2 us
    all_gather x1, waiting for transfers between devices, per_device(): full_spatial = lax.all_gather(latent, 'head', axis=2, tiled=True)  83.4 us
    all_gather x1, waiting for transfers between devices, per_device(): full_stream = lax.all_gather(stream_one, 'head', axis=2, tiled=True)  79.9 us
    all_gather x1, waiting for transfers between devices, per_device(): full_two = lax.all_gather(stream_two, 'head', axis=2, tiled=True)  79 us
    all_to_all x1, blocking collectives, per_device(): lax.all_to_all(stacked, 'seq', split_axis=1, concat_axis=0, tiled=True)  52.9 us
    dot_general x1, matrix products, per_device(): jnp.dot(hidden, output_weight, preferred_element_type=jnp.float32)  27.8 us
  transfers between devices with their start and end apart: 9, of which 8 were waited for; matrix products, arithmetic and copies ran while one was open for 3% of the time, Pallas kernels for 0%

commit v1 on v0

v1 whole, which is shorter than its diff:
```python
import functools
import math

import jax
import jax.numpy as jnp
from jax import lax
from jax.experimental import pallas as pl
from jax.experimental.pallas import tpu as pltpu
from jax.sharding import PartitionSpec as P

HD = 64
PAIR = 128
CHUNKS = 2
EXP2_SCALE = HD ** (-0.5) * math.log2(math.e)
BF16 = jnp.bfloat16
NT = (((1,), (1,)), ((), ()))


def layer_norm(values):
    average = jnp.mean(values, axis=-1, keepdims=True)
    centred = values - average
    variance = jnp.mean(centred * centred, axis=-1, keepdims=True)
    return centred * lax.rsqrt(variance + 1e-06)


def modulate(stream, modulation, offset):
    normed = layer_norm(stream.astype(jnp.float32))
    return (normed * (1.0 + modulation[offset + 1]) + modulation[offset]).astype(BF16)


def weighted_values(scores, values):
    top = jnp.max(scores, axis=-1, keepdims=True)
    weights = jnp.exp2((scores - top) * EXP2_SCALE).astype(BF16)
    extended = jnp.concatenate([values, jnp.ones_like(values)], axis=1)
    summed = jnp.dot(weights, extended, preferred_element_type=jnp.float32)
    return summed[:, :HD] / summed[:, HD:]


def spatial_kernel(q_ref, k_ref, v_ref, o_ref):
    outs = []
    for head in range(PAIR // HD):
        lanes = slice(head * HD, (head + 1) * HD)
        scores = lax.dot_general(
            q_ref[0, :, lanes], k_ref[0, :, lanes], NT, preferred_element_type=jnp.float32
        )
        outs.append(weighted_values(scores, v_ref[0, :, lanes]))
    o_ref[0] = jnp.concatenate(outs, axis=1).astype(BF16)


def spatial_attention(query, keys, values):
    frames, patches, width = query.shape
    rows = min(patches, 512)
    return pl.pallas_call(
        spatial_kernel,
        grid=(frames, width // PAIR, patches // rows),
        in_specs=[
            pl.BlockSpec((1, rows, PAIR), lambda f, h, r: (f, r, h)),
            pl.BlockSpec((1, patches, PAIR), lambda f, h, r: (f, 0, h)),
            pl.BlockSpec((1, patches, PAIR), lambda f, h, r: (f, 0, h)),
        ],
        out_specs=pl.BlockSpec((1, rows, PAIR), lambda f, h, r: (f, r, h)),
        out_shape=jax.ShapeDtypeStruct(query.shape, BF16),
        cost_estimate=pl.CostEstimate(
            flops=16 * frames * patches * patches * width,
            bytes_accessed=8 * query.size,
            transcendentals=frames * patches * patches * (width // HD),
        ),
        name="spatial_attention",
    )(query, keys, values)


def temporal_kernel(q_ref, k_ref, v_ref, o_ref):
    frames, group, width = q_ref.shape
    rows = frames * group
    query = q_ref[...].reshape(rows, width)
    keys = k_ref[...].reshape(rows, width)
    values = v_ref[...].reshape(rows, width)
    first = lax.broadcasted_iota(jnp.int32, (rows, rows), 0)
    second = lax.broadcasted_iota(jnp.int32, (rows, rows), 1)
    same_patch = lax.rem(first, group) == lax.rem(second, group)
    outs = []
    for head in range(width // HD):
        lanes = slice(head * HD, (head + 1) * HD)
        scores = lax.dot_general(
            query[:, lanes], keys[:, lanes], NT, preferred_element_type=jnp.float32
        )
        outs.append(
            weighted_values(jnp.where(same_patch, scores, -jnp.inf), values[:, lanes])
        )
    o_ref[...] = jnp.concatenate(outs, axis=1).astype(BF16).reshape(frames, group, width)


def temporal_attention(query, keys, values):
    frames, patches, width = query.shape
    group = min(16, patches)
    spec = pl.BlockSpec((frames, group, width), lambda g: (0, g, 0))
    return pl.pallas_call(
        temporal_kernel,
        grid=(patches // group,),
        in_specs=[spec] * 3,
        out_specs=spec,
        out_shape=jax.ShapeDtypeStruct(query.shape, BF16),
        cost_estimate=pl.CostEstimate(
            flops=16 * frames * frames * patches * group * width,
            bytes_accessed=8 * query.size,
            transcendentals=frames * frames * patches * group * (width // HD),
        ),
        name="temporal_attention",
    )(query, keys, values)


def project_three(normed, weights):
    return [
        jnp.dot(normed, weights[member], preferred_element_type=jnp.float32).astype(BF16)
        for member in range(3)
    ]


def summed_columns(portion, row_block):
    partial = jnp.dot(portion, row_block, preferred_element_type=jnp.float32).astype(BF16)
    return lax.psum_scatter(partial, "head", scatter_dimension=2, tiled=True)


def add_branch(stream, gate, reduced):
    return (stream.astype(jnp.float32) + gate * reduced.astype(jnp.float32)).astype(BF16)


def per_device(
    latent,
    modulation,
    spatial_qkv,
    spatial_out,
    temporal_qkv,
    temporal_out,
    hidden_weight,
    output_weight,
):
    frames_local, patches, width_local = latent.shape
    seq = lax.axis_size("seq")
    patches_local = patches // seq
    piece = patches_local // CHUNKS
    anchor = lax.axis_index("head") * width_local
    local_rows = lax.dynamic_slice_in_dim(modulation, anchor, width_local, 1)
    full_spatial = lax.all_gather(latent, "head", axis=2, tiled=True)
    normed = modulate(full_spatial, modulation, 0)
    query, keys, values = project_three(normed, spatial_qkv)
    spatial = spatial_attention(query, keys, values)

    def chunk_of(tensor, index):
        parts = tensor.reshape(frames_local, seq, CHUNKS, piece, width_local)
        return parts[:, :, index].reshape(frames_local, seq * piece, width_local)

    outs = []
    ones = []
    for index in range(CHUNKS):
        reduced = summed_columns(chunk_of(spatial, index), spatial_out)
        ones.append(add_branch(chunk_of(latent, index), local_rows[2], reduced))
    ones = [
        lax.all_to_all(one, "seq", split_axis=1, concat_axis=0, tiled=True) for one in ones
    ]
    twos = []
    for one in ones:
        full = lax.all_gather(one, "head", axis=2, tiled=True)
        normed = modulate(full, modulation, 3)
        temporal = temporal_attention(*project_three(normed, temporal_qkv))
        reduced = summed_columns(temporal, temporal_out)
        twos.append(add_branch(one, local_rows[5], reduced))
    for two in twos:
        full = lax.all_gather(two, "head", axis=2, tiled=True)
        normed = modulate(full, modulation, 6)
        pre_act = jnp.dot(normed, hidden_weight, preferred_element_type=jnp.float32)
        hidden = jax.nn.gelu(pre_act, approximate=True).astype(BF16)
        reduced = summed_columns(hidden, output_weight)
        outs.append(add_branch(two, local_rows[8], reduced))
    return jnp.concatenate(outs, axis=1)


def solution(mesh):
    in_specs = (
        P("seq", None, "head"),
        P(),
        P(None, None, "head"),
        P("head", None),
        P(None, None, "head"),
        P("head", None),
        P(None, "head"),
        P("head", None),
    )
    out_specs = P(None, "seq", "head")
    return jax.shard_map(
        per_device, mesh=mesh, in_specs=in_specs, out_specs=out_specs, check_vma=False
    )
```

time: 849 us -> 622 us (0.73)
  waiting for transfers between devices: 598 us -> 402 us
  Pallas kernels: 0 us -> 40.3 us
  local copies, waits for them, and re-layouts: 38 us -> 9.8 us
  blocking collectives: 52.9 us -> 25.3 us
  matrix products: 90 us -> 71.6 us
    all_to_all x3 -> x0, waiting for transfers between devices: 199 us -> none  [the longest x1 100 us: per_device(): lax.all_to_all(spatial_out, 'head', split_axis=1, concat_axis=0, tiled=True)]
    reduce_scatter x1 -> x6, waiting for transfers between devices: 143 us -> 214 us  [summed_columns(): return lax.psum_scatter(partial, 'head', scatter_dimension=2, tiled=True)]
    all_gather x4, waiting for transfers between devices: 171 us -> 102 us  [the longest x2 70 us: per_device(): full = lax.all_gather(two, 'head', axis=2, tiled=True)]
    pallas_call x0 -> x3, Pallas kernels: none -> 40.3 us  [the longest x2 21.6 us: temporal_attention(): pl.pallas_call(temporal_kernel, grid=(patches // group,), in_specs=[spec]...]
    all_to_all x1 -> x2, blocking collectives: 52.9 us -> 25.3 us  [per_device(): lax.all_to_all(one, 'seq', split_axis=1, concat_axis=0, tiled=True)]
    dot_general x6 -> x8, matrix products: 61.2 us -> 45.6 us  [the longest x6 26.5 us: summed_columns(): jnp.dot(portion, row_block, preferred_element_type=jnp.float32).astype(BF16)]
    sub x1 -> x0, matrix products: 14.6 us -> none  [attend(): attn_weights = jax.nn.softmax(scores, axis=-1).astype(jnp.bfloat16)]
    another operation x4 -> x0, local copies, waits for them, and re-layouts: 12.5 us -> none  [the longest x3 9.75 us: to_groups(): tensor.reshape(frames, patches_local, heads_local, HD)]
  transfers between devices with their start and end apart: 9 -> 11, of which waited for: 8 -> 11; matrix products, arithmetic and copies ran while one was open for 3% -> 14% of each run, Pallas kernels for 0% -> 4%
where the time goes in v1:
time: 622 us; the launch traced here: 614 us
  waiting for transfers between devices  402 us (65%)
  matrix products  71.6 us (12%)
  Pallas kernels  40.3 us (6%)
  other arithmetic  39.9 us (6%)
  blocking collectives  25.3 us (4%)
  between operations  13.9 us (2%)
  starting transfers between devices  11 us (2%)
  local copies, waits for them, and re-layouts  9.8 us (2%)
    reduce_scatter x6, waiting for transfers between devices, summed_columns(): return lax.psum_scatter(partial, 'head', scatter_dimension=2, tiled=True)  214 us
    all_gather x1, waiting for transfers between devices, per_device(): full_spatial = lax.all_gather(latent, 'head', axis=2, tiled=True)  84 us
    all_gather x2, waiting for transfers between devices, per_device(): full = lax.all_gather(two, 'head', axis=2, tiled=True)  70 us
    all_gather x2, waiting for transfers between devices, per_device(): full = lax.all_gather(one, 'head', axis=2, tiled=True)  32.4 us
    dot_general x6, matrix products, summed_columns(): jnp.dot(portion, row_block, preferred_element_type=jnp.float32).astype(BF16)  26.5 us
    dot_general x9, matrix products, project_three(): jnp.dot(normed, weights[member], preferred_element_type=jnp.float32)  26.1 us
    all_to_all x2, blocking collectives, per_device(): lax.all_to_all(one, 'seq', split_axis=1, concat_axis=0, tiled=True)  25.3 us
    pallas_call x2, Pallas kernels, temporal_attention(): pl.pallas_call(temporal_kernel, grid=(patches // group,), in_specs=[spec]...  21.6 us
  transfers between devices with their start and end apart: 11, of which 11 were waited for; matrix products, arithmetic and copies ran while one was open for 14% of the time, Pallas kernels for 4%

profile of v1, /device:TPU:0, one launch (start us, length us, event | category | flops | bytes accessed | tf_op | source)
XLA Modules:
  0.0 613.5 jit_solution(17385533944623356714)
XLA Ops:
  6.5 0.7 all-gather.6.cloned.1.call-update
  7.3 1.1 slice_add_fusion
  8.4 84.0 %all-gather.6.cloned.1.call-done = bf16[1,1024,2048]{2,1,0:T(8,128)(2,1)} async-done(((bf16[1,1024,512]{2,1,0:T(8,128)(2,1)}), bf16[1,1024,2048]{2,1,0:T(8,128)(2,1)}) %all-gather.6.cloned.1.call-update) | async-done | bytes 4194320 | tf_op jit(solution)/shard_map/all_gather | solution.py:144
  92.4 3.0 convert_reduce_fusion
  95.4 0.5 copy-done.2
  95.8 1.2 fusion.2
  97.1 1.9 fusion.54
  99.4 3.3 fusion.115.v_ref
  102.7 3.3 fusion.118.k_ref
  106.0 3.3 fusion.121.q_ref
  109.3 18.6 %spatial_attention.1 = bf16[1,1024,512]{2,1,0:T(8,128)(2,1)} custom-call(bf16[1,1024,512]{2,1,0:T(8,128)(2,1)} %fusion.121.q_ref, bf16[1,1024,512]{2,1,0:T(8,128)(2,1)} %fusion.118.k_ref, bf16[1,1024,512]{2,1,0:T(8,128)(2,1)} %fusion.115.v_ref), custom_call_target="tpu_custom_call" | custom-call | flops 8589934592 | bytes 4194304 | tf_op jit(solution)/shard_map/spatial_attention/pallas_call | solution.py:53
  127.9 2.1 fusion.151
  130.0 2.6 fusion.66
  133.0 3.7 fusion.65
  136.8 0.9 fusion.152
  137.8 37.2 %reduce-scatter.13.cloned.1.call-done = bf16[1,512,512]{2,1,0:T(8,128)(2,1)} async-done(((bf16[1,512,2048]{2,1,0:T(8,128)(2,1)}), bf16[1,512,512]{2,1,0:T(8,128)(2,1)}) %reduce-scatter.13.cloned.1.call-update) | async-done | bytes 524304 | tf_op jit(solution)/shard_map/reduce_scatter | solution.py:121
  174.9 45.2 %reduce-scatter.7.cloned.1.call-done = bf16[1,512,512]{2,1,0:T(8,128)(2,1)} async-done(((bf16[1,512,2048]{2,1,0:T(8,128)(2,1)}), bf16[1,512,512]{2,1,0:T(8,128)(2,1)}) %reduce-scatter.7.cloned.1.call-update) | async-done | bytes 524304 | tf_op jit(solution)/shard_map/reduce_scatter | solution.py:121
  220.1 1.5 fusion.143
  221.6 0.8 copy.25
  222.4 0.5 broadcast.163
  222.9 3.8 reduce.3
  227.1 13.2 %all_to_all.24 = bf16[8,2,16384]{2,1,0:T(2,128)(2,1)S(1)} all-to-all(bf16[8,2,16384]{2,1,0:T(2,128)(2,1)S(1)} %reshape.181), channel_id=1, replica_groups=mesh['seq'=8,'head'=4] {'seq'}, dimensions={0} | all-to-all | bytes 1048576 | tf_op jit(solution)/shard_map/all_to_all | solution.py:159
  240.3 0.5 reshape.182
  240.9 0.9 copy.20
  241.9 0.8 copy.26
  242.7 3.8 reduce.2
  246.9 12.1 %all_to_all.25 = bf16[8,2,16384]{2,1,0:T(2,128)(2,1)S(1)} all-to-all(bf16[8,2,16384]{2,1,0:T(2,128)(2,1)S(1)} %reshape.183), channel_id=1, replica_groups=mesh['seq'=8,'head'=4] {'seq'}, dimensions={0} | all-to-all | bytes 1048576 | tf_op jit(solution)/shard_map/all_to_all | solution.py:159
  259.0 0.5 reshape.184
  259.5 0.9 copy.19
  260.5 10.1 %reduce-scatter.15.cloned.1.call-start = ((), (), s32[]{:S(2)}) async-start(), calls=%async_computation.16 | async-start | bytes 2621440 | tf_op jit(solution)/shard_map/reduce_scatter | solution.py:121
  270.6 14.4 %all-gather.12.cloned.1.call-done = bf16[8,64,2048]{2,1,0:T(8,128)(2,1)} async-done(((bf16[8,64,512]{2,1,0:T(8,128)(2,1)}), bf16[8,64,2048]{2,1,0:T(8,128)(2,1)}) %all-gather.12.cloned.1.call-update) | async-done | bytes 2097168 | tf_op jit(solution)/shard_map/all_gather | solution.py:163
  285.0 2.1 convert_reduce_fusion.2
  287.1 2.4 fusion.26
  289.5 3.9 fusion.139.v_ref
  293.4 2.1 fusion.133.k_ref
  295.5 2.1 fusion.127.q_ref
  297.6 10.8 %temporal_attention.3 = bf16[8,64,512]{2,1,0:T(8,128)(2,1)} custom-call(bf16[8,64,512]{2,1,0:T(8,128)(2,1)} %fusion.127.q_ref, bf16[8,64,512]{2,1,0:T(8,128)(2,1)} %fusion.133.k_ref, bf16[8,64,512]{2,1,0:T(8,128)(2,1)} %fusion.139.v_ref), custom_call_target="tpu_custom_call" | custom-call | flops 536870912 | bytes 2097152 | tf_op jit(solution)/shard_map/temporal_attention/pallas_call | solution.py:97
  308.4 4.4 convolution_convert_fusion
  312.9 18.0 %all-gather.8.cloned.1.call-done = bf16[8,64,2048]{2,1,0:T(8,128)(2,1)} async-done(((bf16[8,64,512]{2,1,0:T(8,128)(2,1)}), bf16[8,64,2048]{2,1,0:T(8,128)(2,1)}) %all-gather.8.cloned.1.call-update) | async-done | bytes 2097168 | tf_op jit(solution)/shard_map/all_gather | solution.py:163
  330.9 2.1 convert_reduce_fusion.4
  333.0 2.4 fusion.34
  335.4 3.8 fusion.136.v_ref
  339.3 2.1 fusion.130.k_ref
  341.4 2.1 fusion.124.q_ref
  343.5 10.8 %temporal_attention.2 = bf16[8,64,512]{2,1,0:T(8,128)(2,1)} custom-call(bf16[8,64,512]{2,1,0:T(8,128)(2,1)} %fusion.124.q_ref, bf16[8,64,512]{2,1,0:T(8,128)(2,1)} %fusion.130.k_ref, bf16[8,64,512]{2,1,0:T(8,128)(2,1)} %fusion.136.v_ref), custom_call_target="tpu_custom_call" | custom-call | flops 536870912 | bytes 2097152 | tf_op jit(solution)/shard_map/temporal_attention/pallas_call | solution.py:97
  354.3 4.4 convolution_convert_fusion.2
  358.8 16.7 %reduce-scatter.15.cloned.1.call-done = bf16[8,64,512]{2,1,0:T(8,128)(2,1)} async-done(((bf16[8,64,2048]{2,1,0:T(8,128)(2,1)}), bf16[8,64,512]{2,1,0:T(8,128)(2,1)}) %reduce-scatter.15.cloned.1.call-update) | async-done | bytes 524304 | tf_op jit(solution)/shard_map/reduce_scatter | solution.py:121
  375.5 45.1 %reduce-scatter.9.cloned.1.call-done = bf16[8,64,512]{2,1,0:T(8,128)(2,1)} async-done(((bf16[8,64,2048]{2,1,0:T(8,128)(2,1)}), bf16[8,64,512]{2,1,0:T(8,128)(2,1)}) %reduce-scatter.9.cloned.1.call-update) | async-done | bytes 524304 | tf_op jit(solution)/shard_map/reduce_scatter | solution.py:121
  420.7 2.5 add_convert_fusion.3
  423.2 0.7 all-gather.10.cloned.1.call-update
  424.2 44.0 %all-gather.14.cloned.1.call-done = bf16[8,64,2048]{2,1,0:T(8,128)(2,1)} async-done(((bf16[8,64,512]{2,1,0:T(8,128)(2,1)}), bf16[8,64,2048]{2,1,0:T(8,128)(2,1)}) %all-gather.14.cloned.1.call-update) | async-done | bytes 2097168 | tf_op jit(solution)/shard_map/all_gather | solution.py:169
  468.2 2.1 convert_reduce_fusion.1
  470.3 2.6 fusion.22
  473.0 9.5 %fusion.53 = bf16[8,64,2048]{2,1,0:T(8,128)(2,1)S(1)} fusion(bf16[2048,2048]{1,0:T(8,128)(2,1)} %param.14, bf16[8,64,2048]{2,1,0:T(8,128)(2,1)S(1)} %copy-done.6, f32[8,64]{1,0:T(8,128)S(1)} %add_rsqrt_fusion, f32[8,64]{1,0:T(8,128)S(1)} %broadcast_multiply_fusion, f32[2048]{0:T(1024)S(1)} %bitcast.146, f32[2048]{0:T(1024)S(1)} %bitcast.144), kind=kOutput, calls=%fused_computation.65 | convolution fusion | flops 4310695936 | bytes 12603392 | tf_op jit(solution)/shard_map/dot_general | solution.py:171
  482.5 5.7 fusion.58
  488.3 26.0 %all-gather.10.cloned.1.call-done = bf16[8,64,2048]{2,1,0:T(8,128)(2,1)} async-done(((bf16[8,64,512]{2,1,0:T(8,128)(2,1)}), bf16[8,64,2048]{2,1,0:T(8,128)(2,1)}) %all-gather.10.cloned.1.call-update) | async-done | bytes 2097168 | tf_op jit(solution)/shard_map/all_gather | solution.py:169
  514.3 2.1 convert_reduce_fusion.3
  516.4 2.6 fusion.30
  519.0 9.6 %fusion.45 = bf16[8,64,2048]{2,1,0:T(8,128)(2,1)S(1)} fusion(bf16[2048,2048]{1,0:T(8,128)(2,1)} %param.14, bf16[8,64,2048]{2,1,0:T(8,128)(2,1)S(1)} %copy-done.4, f32[2048]{0:T(1024)S(1)} %bitcast.147, f32[2048]{0:T(1024)S(1)} %bitcast.145, f32[8,64]{1,0:T(8,128)S(1)} %add_rsqrt_fusion.2, f32[8,64]{1,0:T(8,128)S(1)} %broadcast_multiply_fusion.2), kind=kOutput, calls=%fused_computation.57 | convolution fusion | flops 4310695936 | bytes 12603392 | tf_op jit(solution)/shard_map/dot_general | solution.py:171
  528.7 5.7 fusion.55
  534.4 24.5 %reduce-scatter.17.cloned.1.call-done = bf16[8,64,512]{2,1,0:T(8,128)(2,1)} async-done(((bf16[8,64,2048]{2,1,0:T(8,128)(2,1)}), bf16[8,64,512]{2,1,0:T(8,128)(2,1)}) %reduce-scatter.17.cloned.1.call-update) | async-done | bytes 524304 | tf_op jit(solution)/shard_map/reduce_scatter | solution.py:121
  558.9 45.2 %reduce-scatter.11.cloned.1.call-done = bf16[8,64,512]{2,1,0:T(8,128)(2,1)} async-done(((bf16[8,64,2048]{2,1,0:T(8,128)(2,1)}), bf16[8,64,512]{2,1,0:T(8,128)(2,1)}) %reduce-scatter.11.cloned.1.call-update) | async-done | bytes 524304 | tf_op jit(solution)/shard_map/reduce_scatter | solution.py:121
  604.0 1.5 add_convert_fusion.2
  605.6 1.0 pad_maximum_fusion
  (80 shorter events, 2.4 us)
Async XLA Ops:
  6.5 123.5 %copy-start = (bf16[512,2048]{1,0:T(8,128)(2,1)S(1)}, bf16[512,2048]{1,0:T(8,128)(2,1)}, u32[]{:S(2)}) copy-start(bf16[512,2048]{1,0:T(8,128)(2,1)} %param.11) | copy-start | bytes 6291460
  6.5 85.9 %all-gather.6.cloned.1.call-start = ((), (), s32[]{:S(2)}) async-start(), calls=%async_computation.8 | async-start | bytes 5242880 | tf_op jit(solution)/shard_map/all_gather | solution.py:144
  7.3 167.7 %reduce-scatter.13.cloned.1.call-start = ((), (), s32[]{:S(2)}) async-start(), calls=%async_computation.14 | async-start | bytes 2621440 | tf_op jit(solution)/shard_map/reduce_scatter | solution.py:121
  92.4 3.4 copy-start.2
  95.8 3.1 slice-start.4
  97.1 2.3 slice-start.5
  132.7 87.4 %reduce-scatter.7.cloned.1.call-start = ((), (), s32[]{:S(2)}) async-start(), calls=%async_computation.9 | async-start | bytes 2621440 | tf_op jit(solution)/shard_map/reduce_scatter | solution.py:121
  133.0 4.7 copy-start.11
  136.7 148.3 %all-gather.12.cloned.1.call-start = ((), (), s32[]{:S(2)}) async-start(), calls=%async_computation.15 | async-start | bytes 2621440 | tf_op jit(solution)/shard_map/all_gather | solution.py:163
  241.8 89.1 %all-gather.8.cloned.1.call-start = ((), (), s32[]{:S(2)}) async-start(), calls=%async_computation.10 | async-start | bytes 2621440 | tf_op jit(solution)/shard_map/all_gather | solution.py:163
  260.5 115.0 %reduce-scatter.15.cloned.1.call-start = ((), (), s32[]{:S(2)}) async-start(), calls=%async_computation.16 | async-start | bytes 2621440 | tf_op jit(solution)/shard_map/reduce_scatter | solution.py:121
  285.0 4.5 copy-start.5
  287.1 6.3 %slice-start.6 = ((s8[6291456]{0:T(1024)(128)(4,1)}), s8[4194304]{0:T(1024)(128)(4,1)S(1)}, s32[]{:S(2)}) async-start(s8[6291456]{0:T(1024)(128)(4,1)} %bitcast.169), calls=%async_computation.25 | async-start | bytes 8388608
  289.5 3.9 slice-start.7
  312.8 107.8 %reduce-scatter.9.cloned.1.call-start = ((), (), s32[]{:S(2)}) async-start(), calls=%async_computation.11 | async-start | bytes 2621440 | tf_op jit(solution)/shard_map/reduce_scatter | solution.py:121
  330.9 4.5 copy-start.3
  333.0 6.3 %slice-start.8 = ((s8[6291456]{0:T(1024)(128)(4,1)}), s8[4194304]{0:T(1024)(128)(4,1)S(1)}, s32[]{:S(2)}) async-start(s8[6291456]{0:T(1024)(128)(4,1)} %bitcast.171), calls=%async_computation.27 | async-start | bytes 8388608
  335.4 3.9 slice-start.9
  354.3 66.3 %copy-start.7 = (bf16[1,512,512]{2,1,0:T(8,128)(2,1)S(1)}, bf16[1,512,512]{2,1,0:T(8,128)(2,1)}, u32[]{:S(2)}) copy-start(bf16[1,512,512]{2,1,0:T(8,128)(2,1)} %copy.20) | copy-start | bytes 1572868
  354.3 66.3 %copy-start.8 = (bf16[1,512,512]{2,1,0:T(8,128)(2,1)S(1)}, bf16[1,512,512]{2,1,0:T(8,128)(2,1)}, u32[]{:S(2)}) copy-start(bf16[1,512,512]{2,1,0:T(8,128)(2,1)} %copy.19) | copy-start | bytes 1572868
  358.8 109.4 %all-gather.14.cloned.1.call-start = ((), (), s32[]{:S(2)}) async-start(), calls=%async_computation.17 | async-start | bytes 2621440 | tf_op jit(solution)/shard_map/all_gather | solution.py:169
  423.2 91.1 %all-gather.10.cloned.1.call-start = ((), (), s32[]{:S(2)}) async-start(), calls=%async_computation.12 | async-start | bytes 2621440 | tf_op jit(solution)/shard_map/all_gather | solution.py:169
  423.9 134.9 %reduce-scatter.17.cloned.1.call-start = ((), (), s32[]{:S(2)}) async-start(), calls=%async_computation.18 | async-start | bytes 2621440 | tf_op jit(solution)/shard_map/reduce_scatter | solution.py:121
  468.2 4.8 copy-start.6
  468.2 14.3 %slice-start = ((s8[8388608]{0:T(1024)(128)(4,1)}), s8[4194304]{0:T(1024)(128)(4,1)S(1)}, s32[]{:S(2)}) async-start(s8[8388608]{0:T(1024)(128)(4,1)} %bitcast.163), calls=%async_computation.19 | async-start | bytes 8388608
  473.0 9.5 %slice-start.1 = ((s8[8388608]{0:T(1024)(128)(4,1)}), s8[4194304]{0:T(1024)(128)(4,1)S(1)}, s32[]{:S(2)}) async-start(s8[8388608]{0:T(1024)(128)(4,1)} %bitcast.163), calls=%async_computation.20 | async-start | bytes 8388608
  488.2 115.8 %reduce-scatter.11.cloned.1.call-start = ((), (), s32[]{:S(2)}) async-start(), calls=%async_computation.13 | async-start | bytes 2621440 | tf_op jit(solution)/shard_map/reduce_scatter | solution.py:121
  514.3 4.7 copy-start.4
  514.3 14.4 %slice-start.2 = ((s8[8388608]{0:T(1024)(128)(4,1)}), s8[4194304]{0:T(1024)(128)(4,1)S(1)}, s32[]{:S(2)}) async-start(s8[8388608]{0:T(1024)(128)(4,1)} %bitcast.165), calls=%async_computation.21 | async-start | bytes 8388608
  519.0 9.6 %slice-start.3 = ((s8[8388608]{0:T(1024)(128)(4,1)}), s8[4194304]{0:T(1024)(128)(4,1)S(1)}, s32[]{:S(2)}) async-start(s8[8388608]{0:T(1024)(128)(4,1)} %bitcast.165), calls=%async_computation.22 | async-start | bytes 8388608
  528.7 75.4 %copy-start.9 = (bf16[8,64,512]{2,1,0:T(8,128)(2,1)S(1)}, bf16[8,64,512]{2,1,0:T(8,128)(2,1)}, u32[]{:S(2)}) copy-start(bf16[8,64,512]{2,1,0:T(8,128)(2,1)} %get-tuple-element.20) | copy-start | bytes 1572868
  528.7 75.4 %copy-start.10 = (bf16[8,64,512]{2,1,0:T(8,128)(2,1)S(1)}, bf16[8,64,512]{2,1,0:T(8,128)(2,1)}, u32[]{:S(2)}) copy-start(bf16[8,64,512]{2,1,0:T(8,128)(2,1)} %get-tuple-element.21) | copy-start | bytes 1572868
  528.7 77.9 %copy-start.1 = (bf16[512,2048]{1,0:T(8,128)(2,1)S(1)}, bf16[512,2048]{1,0:T(8,128)(2,1)}, u32[]{:S(2)}) copy-start(bf16[512,2048]{1,0:T(8,128)(2,1)} %param.11) | copy-start | bytes 6291460
Sparse Core Ops, SparseCore 0:
  8.9 83.4 all-gather.5
  132.8 42.1 reduce-scatter.12
  177.2 42.8 reduce-scatter.6
  241.9 43.0 all-gather.11
  286.4 44.4 all-gather.7
  333.0 42.4 reduce-scatter.14
  377.8 42.8 reduce-scatter.8
  423.3 44.8 all-gather.13
  469.8 44.4 all-gather.9
  516.4 42.4 reduce-scatter.16
  561.2 42.8 reduce-scatter.10
